TPU v7x, 32 devices: a whole 2x2x4 slice. The times are simulated.
32 devices in a mesh: tp: 8 (over y, x, core), col: 4 (over z).
Axes of the slice: x: 2, y: 2, z: 4, core: 2. Of those that a mesh axis runs over, the one named last changes fastest.
Arguments:
- gate_in: bfloat16 [128, 53248], P('col', 'tp'), may hold values from -6 to 6
- up_in: bfloat16 [128, 53248], P('col', 'tp'), may hold values from -6 to 6
- down_weight: bfloat16 [53248, 16384], P('tp', 'col'), may hold values from -0.02734375 to 0.02734375
- residual: bfloat16 [128, 16384], P('tp', 'col'), may hold values from -30 to 30
- norm_gain: bfloat16 [16384], P('col'), may hold values from 0.5 to 1.5
Outputs:
- stream: bfloat16 [128, 16384], P('tp', 'col')
- normed: bfloat16 [128, 16384], P('tp', 'col')
All inputs are finite; a program needn't handle non-finite values.
Results may differ from a plain program's by a relative error of at most 0.0034.
Values may be sent and summed in bfloat16 or wider, within the bound.
A program may use at most 128 MiB of HBM per device.

v0:
```python
import functools

import jax
import jax.numpy as jnp
from jax import lax
from jax.experimental import pallas as pl
from jax.experimental.pallas import tpu as pltpu
from jax.sharding import PartitionSpec as P

MESH = pl.DeviceIdType.MESH
VMEM_BYTES = 67_043_328
EPS = 1e-05


def gated(gate_part, up_part):
    return (jax.nn.silu(gate_part.astype(jnp.float32)) * up_part.astype(jnp.float32)).astype(
        jnp.bfloat16
    )


def plain_body(width, gate_in, up_in, down_weight, residual, norm_gain):
    local_act = gated(gate_in, up_in)
    hidden = lax.all_gather(local_act, "col", axis=0, tiled=True)
    partial_value = jnp.dot(hidden, down_weight, preferred_element_type=jnp.float32)
    branch = lax.psum_scatter(partial_value, "tp", scatter_dimension=0, tiled=True)
    summed = residual.astype(jnp.float32) + branch
    local_squares = jnp.sum(summed * summed, axis=1, keepdims=True)
    mean_square = lax.psum(local_squares, "col") / width
    scaled = summed * lax.rsqrt(mean_square + EPS) * norm_gain.astype(jnp.float32)[None, :]
    return (summed.astype(jnp.bfloat16), scaled.astype(jnp.bfloat16))


def pick(extent, most, step):
    best = 0
    for size in range(step, min(extent, most) + 1, step):
        if extent % size == 0:
            best = size
    return best


def kernel(
    n_col, n_pair, kp, nt, rt, skew,
    gate_hbm, up_hbm, w_hbm, res_hbm,
    out_hbm, sq_out,
    gate_v, up_v, hid, w_v, acc, peer, send_buf, recv_buf, own, res_v, total, squares,
    in_sem, w_sem, res_sem, out_sem, ag_send, ag_recv, d_send, d_recv, r_send, r_recv, q_send, q_recv,
):
    rows, depth = gate_hbm.shape
    width = w_hbm.shape[1]
    pieces = depth // kp
    tiles = width // rt
    me = lax.axis_index("tp")
    z = lax.axis_index("col")
    plane, core = me // 2, lax.rem(me, 2)

    barrier = pltpu.get_barrier_semaphore()
    for step in range(1, n_col):
        pl.semaphore_signal(
            barrier, inc=1, device_id={"col": lax.rem(z + step, n_col)}, device_id_type=MESH
        )
    pl.semaphore_signal(barrier, inc=1, device_id={"tp": 2 * plane + 1 - core}, device_id_type=MESH)
    for step in range(1, n_pair):
        pl.semaphore_signal(
            barrier,
            inc=1,
            device_id={"tp": 2 * lax.rem(plane + step, n_pair) + core},
            device_id_type=MESH,
        )

    def cols(s):
        return pl.ds(pl.multiple_of(s * kp, kp), kp)

    def load(s, which):
        src, dst = ((gate_hbm, gate_v), (up_hbm, up_v))[which]
        return pltpu.make_async_copy(src.at[:, cols(s)], dst.at[:, cols(s)], in_sem.at[which, s])

    def load_w(s):
        return pltpu.make_async_copy(w_hbm.at[cols(s), :], w_v.at[cols(s), :], w_sem.at[s])

    load_res = pltpu.make_async_copy(res_hbm, res_v, res_sem)

    @pl.loop(0, pieces)
    def _(s):
        load(s, 0).start()
        load(s, 1).start()

    @pl.loop(0, pieces)
    def _(s):
        load_w(s).start()

    load_res.start()

    def hid_rows(source):
        return pl.ds(pl.multiple_of(source * rows, rows), rows)

    def hop(source, s, up):
        block = hid.at[hid_rows(source), cols(s)]
        return pltpu.make_async_remote_copy(
            src_ref=block,
            dst_ref=block,
            send_sem=ag_send.at[0 if up else 1, source],
            recv_sem=ag_recv.at[source, s],
            device_id={"col": z + 1 if up else z - 1},
            device_id_type=MESH,
        )

    def send_both(source, s):
        @pl.when(z < n_col - 1)
        def _():
            hop(source, s, True).start()

        @pl.when(z > 0)
        def _():
            hop(source, s, False).start()

    pl.semaphore_wait(barrier, n_col - 1 + 1 + n_pair - 1)

    @pl.loop(0, pieces + 1)
    def _(s):
        @pl.when(s < pieces)
        def _():
            load(s, 0).wait()
            load(s, 1).wait()
            g = gate_v[:, cols(s)].astype(jnp.float32)
            u = up_v[:, cols(s)].astype(jnp.float32)
            hid[hid_rows(z), cols(s)] = (g / (1.0 + jnp.exp(-g)) * u).astype(jnp.bfloat16)

        @pl.when(s > 0)
        def _():
            send_both(z, s - 1)

    acc[...] = jnp.zeros_like(acc)

    @pl.loop(0, pieces + skew * (n_col - 2))
    def _(i):
        for away in range(n_col - 1, 0, -1):
            s = i - skew * (away - 1)
            live = jnp.logical_and(s >= 0, s < pieces)

            @pl.when(jnp.logical_and(live, z - away >= 0))
            def _():
                hop(z - away, s, True).wait_recv()

                @pl.when(z < n_col - 1)
                def _():
                    hop(z - away, s, True).start()

            @pl.when(jnp.logical_and(live, z + away < n_col))
            def _():
                hop(z + away, s, False).wait_recv()

                @pl.when(z > 0)
                def _():
                    hop(z + away, s, False).start()

        s = i - skew * (n_col - 2)

        @pl.when(s >= 0)
        def _():
            load_w(s).wait()
            a = hid[:, cols(s)]
            for n in range(width // nt):
                part = jnp.dot(
                    a, w_v[cols(s), n * nt : (n + 1) * nt], preferred_element_type=jnp.float32
                )
                acc[:, :, :, n * nt : (n + 1) * nt] += part.reshape(acc.shape[:3] + (nt,))

    def swap(n):
        return pltpu.make_async_remote_copy(
            src_ref=acc.at[:, 1 - core, :, n * rt : (n + 1) * rt],
            dst_ref=peer.at[:, :, n * rt : (n + 1) * rt],
            send_sem=d_send,
            recv_sem=d_recv.at[n],
            device_id={"tp": 2 * plane + 1 - core},
            device_id_type=MESH,
        )

    def scatter(n, step):
        to = lax.rem(plane + step, n_pair)
        return pltpu.make_async_remote_copy(
            src_ref=send_buf.at[to, :, n * rt : (n + 1) * rt],
            dst_ref=recv_buf.at[step - 1, :, n * rt : (n + 1) * rt],
            send_sem=r_send.at[step - 1],
            recv_sem=r_recv.at[step - 1, n],
            device_id={"tp": 2 * to + core},
            device_id_type=MESH,
        )

    for n in range(tiles):
        swap(n).start()
    load_res.wait()
    for n in range(tiles + 1):
        if n < tiles:
            here = slice(n * rt, (n + 1) * rt)
            swap(n).wait_recv()
            both = acc[:, core, :, here] + peer[:, :, here]
            send_buf[:, :, here] = both.astype(jnp.bfloat16)
            own[:, here] = (
                acc[plane, core, :, here] + peer[plane, :, here]
                + res_v[:, here].astype(jnp.float32)
            )
        if n > 0:
            for step in range(1, n_pair):
                scatter(n - 1, step).start()

    sums = jnp.zeros((res_hbm.shape[0], 128), jnp.float32)
    writes = []
    for n in range(tiles):
        here = slice(n * rt, (n + 1) * rt)
        value = own[:, here]
        for step in range(1, n_pair):
            scatter(n, step).wait_recv()
            value = value + recv_buf[step - 1, :, here].astype(jnp.float32)
        total[:, here] = value
        square = value * value
        for j in range(rt // 128):
            sums = sums + square[:, j * 128 : (j + 1) * 128]
        write = pltpu.make_async_copy(total.at[:, here], out_hbm.at[:, here], out_sem.at[n])
        write.start()
        writes.append(write)

    squares[z] = jnp.broadcast_to(jnp.sum(sums, axis=1, keepdims=True), sums.shape)

    def share(step):
        return pltpu.make_async_remote_copy(
            src_ref=squares.at[z],
            dst_ref=squares.at[z],
            send_sem=q_send.at[step - 1],
            recv_sem=q_recv.at[step - 1],
            device_id={"col": lax.rem(z + step, n_col)},
            device_id_type=MESH,
        )

    def arrival(step):
        block = squares.at[lax.rem(z + n_col - step, n_col)]
        return pltpu.make_async_remote_copy(
            src_ref=block,
            dst_ref=block,
            send_sem=q_send.at[step - 1],
            recv_sem=q_recv.at[step - 1],
            device_id={"col": lax.rem(z + step, n_col)},
            device_id_type=MESH,
        )

    for step in range(1, n_col):
        share(step).start()

    for source in range(n_col):
        block = hid.at[source * rows : (source + 1) * rows, :]
        for up in (0, 1):
            sent = jnp.logical_and(source <= z, z < n_col - 1)
            if not up:
                sent = jnp.logical_and(source >= z, z > 0)

            @pl.when(sent)
            def _():
                pltpu.make_async_remote_copy(
                    src_ref=block,
                    dst_ref=block,
                    send_sem=ag_send.at[0 if up else 1, source],
                    recv_sem=ag_recv.at[source, 0],
                    device_id={"col": z + 1 if up else z - 1},
                    device_id_type=MESH,
                ).wait_send()

    pltpu.make_async_remote_copy(
        src_ref=peer,
        dst_ref=peer,
        send_sem=d_send,
        recv_sem=d_recv.at[0],
        device_id={"tp": 2 * plane + 1 - core},
        device_id_type=MESH,
    ).wait_send()
    for step in range(1, n_pair):
        to = lax.rem(plane + step, n_pair)
        pltpu.make_async_remote_copy(
            src_ref=send_buf.at[to],
            dst_ref=recv_buf.at[step - 1],
            send_sem=r_send.at[step - 1],
            recv_sem=r_recv.at[step - 1, 0],
            device_id={"tp": 2 * to + core},
            device_id_type=MESH,
        ).wait_send()
    for write in writes:
        write.wait()
    for step in range(1, n_col):
        share(step).wait_send()
        arrival(step).wait_recv()
    whole = squares[0]
    for j in range(1, n_col):
        whole = whole + squares[j]
    sq_out[...] = whole


def fused_body(n_tp, n_col, kp, nt, rt, width, gate_in, up_in, down_weight, residual, norm_gain):
    rows, depth = gate_in.shape
    local = down_weight.shape[1]
    own_rows = residual.shape[0]
    n_pair = n_tp // 2
    pieces, tiles = depth // kp, local // rt
    any_space = pl.BlockSpec(memory_space=pl.ANY)
    dma = pltpu.SemaphoreType.DMA
    summed, squares = pl.pallas_call(
        functools.partial(kernel, n_col, n_pair, kp, nt, rt, min(3, pieces)),
        out_shape=(
            jax.ShapeDtypeStruct((own_rows, local), jnp.float32),
            jax.ShapeDtypeStruct((own_rows, 128), jnp.float32),
        ),
        in_specs=[any_space] * 4,
        out_specs=(any_space, pl.BlockSpec(memory_space=pltpu.VMEM)),
        scratch_shapes=[
            pltpu.VMEM((rows, depth), jnp.bfloat16),
            pltpu.VMEM((rows, depth), jnp.bfloat16),
            pltpu.VMEM((rows * n_col, depth), jnp.bfloat16),
            pltpu.VMEM((depth, local), jnp.bfloat16),
            pltpu.VMEM((n_pair, 2, own_rows, local), jnp.float32),
            pltpu.VMEM((n_pair, own_rows, local), jnp.float32),
            pltpu.VMEM((n_pair, own_rows, local), jnp.bfloat16),
            pltpu.VMEM((n_pair - 1, own_rows, local), jnp.bfloat16),
            pltpu.VMEM((own_rows, local), jnp.float32),
            pltpu.VMEM((own_rows, local), jnp.bfloat16),
            pltpu.VMEM((own_rows, local), jnp.float32),
            pltpu.VMEM((n_col, own_rows, 128), jnp.float32),
            dma((2, pieces)),
            dma((pieces,)),
            dma,
            dma((tiles,)),
            dma((2, n_col)),
            dma((n_col, pieces)),
            dma,
            dma((tiles,)),
            dma((n_pair - 1,)),
            dma((n_pair - 1, tiles)),
            dma((n_col - 1,)),
            dma((n_col - 1,)),
        ],
        compiler_params=pltpu.CompilerParams(
            collective_id=0, has_side_effects=True, vmem_limit_bytes=VMEM_BYTES
        ),
        name="down_reduce",
    )(gate_in, up_in, down_weight, residual)
    mean_square = squares[:, :1] / width
    scaled = summed * lax.rsqrt(mean_square + EPS) * norm_gain.astype(jnp.float32)[None, :]
    return (summed.astype(jnp.bfloat16), scaled.astype(jnp.bfloat16))


def pairs_share_chip(mesh):
    if tuple(mesh.axis_names) != ("tp", "col") or mesh.shape["tp"] % 2 or mesh.shape["tp"] < 4:
        return False
    devices = mesh.devices
    for j in range(0, mesh.shape["tp"], 2):
        for a, b in zip(devices[j], devices[j + 1]):
            first = getattr(a, "coords", None)
            if first is None or list(first) != list(getattr(b, "coords", ())):
                return False
    return True


def solution(mesh):
    in_specs = (P("col", "tp"), P("col", "tp"), P("tp", "col"), P("tp", "col"), P("col"))
    out_specs = (P("tp", "col"), P("tp", "col"))
    n_tp, n_col = mesh.shape["tp"], mesh.shape["col"]

    def run(gate_in, up_in, down_weight, residual, norm_gain):
        tokens, hidden_units = gate_in.shape
        width = down_weight.shape[1]
        depth, local = hidden_units // n_tp, width // n_col
        rows, own_rows = tokens // n_col, tokens // n_tp
        kp, nt, rt = pick(depth, 512, 128), pick(local, 1024, 128), pick(local, 512, 128)
        need = 2 * depth * (local + tokens + 2 * rows) + local * tokens * 9 + (4 << 20)
        fused = (
            pairs_share_chip(mesh)
            and n_col > 1
            and rows % 16 == 0
            and own_rows % 16 == 0
            and kp > 0
            and nt > 0
            and need < VMEM_BYTES
        )
        body = functools.partial(plain_body, width)
        if fused:
            body = functools.partial(fused_body, n_tp, n_col, kp, nt, rt, width)
        return jax.shard_map(
            body, mesh=mesh, in_specs=in_specs, out_specs=out_specs, check_vma=False
        )(gate_in, up_in, down_weight, residual, norm_gain)

    return run
```

profile of v0, /device:TPU:1, one launch (start us, length us, event | category | flops | bytes accessed | tf_op | source)
XLA Modules:
  0.0 53.6 jit_solution(18446219937844426578)
XLA Ops:
  0.6 1.3 %convert_element_type.10 = f32[4096]{0:T(1024)} convert(bf16[4096]{0:T(1024)(128)(2,1)} %param.9) | non-fusion elementwise | flops 4096 | bytes 24576 | tf_op jit(solution)/shard_map/convert_element_type | solution.py:343
  1.9 49.1 %down_reduce.1 = (f32[16,4096]{1,0:T(8,128)}, f32[16,128]{1,0:T(8,128)}) custom-call(bf16[32,6656]{1,0:T(8,128)(2,1)} %gate_hbm.1, bf16[32,6656]{1,0:T(8,128)(2,1)} %up_hbm.1, bf16[6656,4096]{1,0:T(8,128)(2,1)} %w_hbm.1, bf16[16,4096]{1,0:T(8,128)(2,1)} %res_hbm.1), custom_call_target="tpu_custom_call" | custom-call | tf_op jit(solution)/shard_map/down_reduce/pallas_call | solution.py:303
  51.0 0.8 %rsqrt_reduce_fusion = f32[16]{0:T(128)S(1)} fusion(f32[16,128]{1,0:T(8,128)} %get-tuple-element.5), kind=kLoop, calls=%fused_computation.1 | loop fusion | flops 32 | bytes 128 | tf_op jit(solution)/shard_map/rsqrt | solution.py:343
  51.8 1.8 %multiply_convert_fusion = (bf16[16,4096]{1,0:T(8,128)(2,1)}, bf16[16,4096]{1,0:T(8,128)(2,1)}) fusion(f32[16,4096]{1,0:T(8,128)} %get-tuple-element.4, f32[4096]{0:T(1024)} %convert_element_type.10, f32[16]{0:T(128)S(1)} %rsqrt_reduce_fusion), kind=kLoop, calls=%fused_computation | loop fusion | flops 262144 | bytes 540736 | tf_op jit(solution)/shard_map/convert_element_type | solution.py:344
where the time goes:
time: 54.2 us; the launch traced here: 53.6 us
  Pallas kernels  49.1 us (91%)
  other arithmetic  3.9 us (7%)
  between operations  0.64 us (1%)
    pallas_call x1, Pallas kernels, fused_body(): pl.pallas_call(functools.partial(kernel, n_col, n_pair, kp, nt, rt, min(3...  49.1 us
    convert_element_type x1, other arithmetic, fused_body(): return (summed.astype(jnp.bfloat16), scaled.astype(jnp.bfloat16))  1.79 us
    convert_element_type x1, other arithmetic, fused_body(): norm_gain.astype(jnp.float32)[None, :]  1.3 us

commit v1 on v0

v1 whole, which is shorter than its diff:
```python
import functools

import jax
import jax.numpy as jnp
from jax import lax
from jax.experimental import pallas as pl
from jax.experimental.pallas import tpu as pltpu
from jax.sharding import PartitionSpec as P

MESH = pl.DeviceIdType.MESH
VMEM_BYTES = 67_043_328
EPS = 1e-05
SKEW = 5
SPLIT = 5


def gated(gate_part, up_part):
    return (jax.nn.silu(gate_part.astype(jnp.float32)) * up_part.astype(jnp.float32)).astype(
        jnp.bfloat16
    )


def plain_body(width, gate_in, up_in, down_weight, residual, norm_gain):
    local_act = gated(gate_in, up_in)
    hidden = lax.all_gather(local_act, "col", axis=0, tiled=True)
    partial_value = jnp.dot(hidden, down_weight, preferred_element_type=jnp.float32)
    branch = lax.psum_scatter(partial_value, "tp", scatter_dimension=0, tiled=True)
    summed = residual.astype(jnp.float32) + branch
    local_squares = jnp.sum(summed * summed, axis=1, keepdims=True)
    mean_square = lax.psum(local_squares, "col") / width
    scaled = summed * lax.rsqrt(mean_square + EPS) * norm_gain.astype(jnp.float32)[None, :]
    return (summed.astype(jnp.bfloat16), scaled.astype(jnp.bfloat16))


def pick(extent, most, step):
    best = 0
    for size in range(step, min(extent, most) + 1, step):
        if extent % size == 0:
            best = size
    return best


def kernel(
    n_col, n_pair, kp, nt, rt, skew, split, width_all,
    gate_hbm, up_hbm, w_hbm, res_hbm, gain_hbm,
    total_hbm, pre_hbm, scale_out,
    gate_v, up_v, hid, w_v, acc, peer, send_buf, recv_buf, total, pre, res_v, gain_v, squares,
    in_sem, w_sem, res_sem, gain_sem, out_sem,
    ag_send, ag_recv, d_send, d_recv, r_send, r_recv, q_send, q_recv,
):
    depth = gate_hbm.shape[1]
    width = w_hbm.shape[1]
    half = res_hbm.shape[0]
    pieces = depth // kp
    whole_units = pieces - split
    units = pieces + split
    tiles = width // rt
    me = lax.axis_index("tp")
    z = lax.axis_index("col")
    plane, core = me // 2, lax.rem(me, 2)

    barrier = pltpu.get_barrier_semaphore()
    for step in range(1, n_col):
        pl.semaphore_signal(
            barrier, inc=1, device_id={"col": lax.rem(z + step, n_col)}, device_id_type=MESH
        )
    pl.semaphore_signal(barrier, inc=1, device_id={"tp": 2 * plane + 1 - core}, device_id_type=MESH)
    for step in range(1, n_pair):
        pl.semaphore_signal(
            barrier,
            inc=1,
            device_id={"tp": 2 * lax.rem(plane + step, n_pair) + core},
            device_id_type=MESH,
        )

    def cols(s):
        return pl.ds(pl.multiple_of(s * kp, kp), kp)

    def load(s, which):
        src, dst = ((gate_hbm, gate_v), (up_hbm, up_v))[which]
        return pltpu.make_async_copy(src.at[:, cols(s)], dst.at[:, cols(s)], in_sem.at[which, s])

    def load_w(s):
        return pltpu.make_async_copy(w_hbm.at[cols(s), :], w_v.at[cols(s), :], w_sem.at[s])

    load_res = pltpu.make_async_copy(res_hbm, res_v, res_sem)
    load_gain = pltpu.make_async_copy(gain_hbm, gain_v, gain_sem)

    @pl.loop(0, pieces)
    def _(s):
        load(s, 0).start()
        load(s, 1).start()

    @pl.loop(0, pieces)
    def _(s):
        load_w(s).start()

    load_res.start()
    load_gain.start()

    def source_rows(source):
        return pl.ds(pl.multiple_of(source * half, half), half)

    def hop(source, group, s, to):
        block = hid.at[group, source_rows(source), cols(s)]
        return pltpu.make_async_remote_copy(
            src_ref=block,
            dst_ref=block,
            send_sem=ag_send.at[(1 + to) // 2, source],
            recv_sem=ag_recv.at[source, group, s],
            device_id={"col": z + to},
            device_id_type=MESH,
        )

    def unit(u):
        group = (u >= pieces).astype(jnp.int32)
        return group, u - split * group

    def each(source, u, to, action):
        group, s = unit(u)
        action(hop(source, group, s, to))

        @pl.when(u < whole_units)
        def _():
            action(hop(source, 1, s, to))

    def start(copy):
        copy.start()

    def pass_on(source, u, to, forward):
        each(source, u, to, lambda copy: copy.wait_recv())

        @pl.when(forward)
        def _():
            each(source, u, to, start)

    below, above = z, n_col - 1 - z
    few, many = jnp.minimum(below, above), jnp.maximum(below, above)
    inward = jnp.where(below < above, 1, -1)
    lag = skew * jnp.maximum(many - 1, 0)
    lead = jnp.where(few > 0, skew, pieces)

    pl.semaphore_wait(barrier, n_col - 1 + 1 + n_pair - 1)

    @pl.loop(0, pieces + 1)
    def _(s):
        @pl.when(s < pieces)
        def _():
            load(s, 0).wait()
            load(s, 1).wait()
            g = gate_v[:, cols(s)].astype(jnp.float32)
            u = up_v[:, cols(s)].astype(jnp.float32)
            h = (g / (1.0 + jnp.exp(-g)) * u).astype(jnp.bfloat16)
            hid[0, source_rows(z), cols(s)] = h[:half]
            hid[1, source_rows(z), cols(s)] = h[half:]

        @pl.when(s > 0)
        def _():
            u = s - 1

            @pl.when(u < lead)
            def _():
                each(z, u, inward, start)

            @pl.when(few > 0)
            def _():
                each(z, u, -inward, start)

    acc[...] = jnp.zeros_like(acc)

    def swap(group, n):
        here = pl.ds(n * rt, rt)
        return pltpu.make_async_remote_copy(
            src_ref=acc.at[group, :, :, here],
            dst_ref=peer.at[:, :, here],
            send_sem=d_send,
            recv_sem=d_recv.at[n],
            device_id={"tp": 2 * plane + 1 - core},
            device_id_type=MESH,
        )

    def scatter(n, step):
        to = lax.rem(plane + step, n_pair)
        here = pl.ds(n * rt, rt)
        return pltpu.make_async_remote_copy(
            src_ref=send_buf.at[to, :, here],
            dst_ref=recv_buf.at[step - 1, :, here],
            send_sem=r_send.at[step - 1],
            recv_sem=r_recv.at[step - 1, n],
            device_id={"tp": 2 * to + core},
            device_id_type=MESH,
        )

    def sum_pair(group):
        for n in range(tiles + 1):
            if n < tiles:
                here = slice(n * rt, (n + 1) * rt)
                swap(group, n).wait_recv()
                send_buf[:, :, here] = (acc[group, :, :, here] + peer[:, :, here]).astype(
                    jnp.bfloat16
                )
                total[:, here] = (
                    acc[group, plane, :, here]
                    + peer[plane, :, here]
                    + res_v[:, here].astype(jnp.float32)
                )
            if n > 0:
                for step in range(1, n_pair):
                    scatter(n - 1, step).start()

    @pl.loop(0, units + skew * (n_col - 2))
    def _(i):
        for away in range(1, (n_col + 1) // 2):

            @pl.when(jnp.logical_and(few >= away, i < units))
            def _():
                pass_on(z - inward * away, i, inward, True)

        mine = i + lead

        @pl.when(mine < units)
        def _():
            each(z, mine, inward, start)

        u = i - lag
        live = jnp.logical_and(u >= 0, u < units)
        for away in range(1, n_col):

            @pl.when(jnp.logical_and(live, many >= away))
            def _():
                pass_on(z + inward * away, u, -inward, few > 0)

        @pl.when(jnp.logical_and(jnp.logical_and(u >= pieces, u < units), few > 0))
        def _():
            each(z, u, -inward, start)

        @pl.when(jnp.logical_and(u == pieces, core == 1))
        def _():
            for n in range(tiles):
                swap(0, n).start()

        @pl.when(jnp.logical_and(u >= 0, u < pieces))
        def _():
            load_w(u).wait()

        @pl.when(jnp.logical_and(u >= 0, u < whole_units))
        def _():
            a = hid[:, :, cols(u)].reshape(2 * n_col * half, kp)
            for n in range(width // nt):
                here = slice(n * nt, (n + 1) * nt)
                part = jnp.dot(a, w_v[cols(u), here], preferred_element_type=jnp.float32)
                acc[:, :, :, here] += part.reshape(2, n_pair, half, nt)

        @pl.when(jnp.logical_and(u >= whole_units, u < units - 1))
        def _():
            group, s = unit(u)
            a = hid[group, :, cols(s)]
            for n in range(width // nt):
                here = slice(n * nt, (n + 1) * nt)
                part = jnp.dot(a, w_v[cols(s), here], preferred_element_type=jnp.float32)
                acc[group, :, :, here] += part.reshape(n_pair, half, nt)

        @pl.when(jnp.logical_and(u == pieces + split // 2 + 1, core == 0))
        def _():
            load_res.wait()
            load_gain.wait()
            sum_pair(0)

    last = pl.ds((pieces - 1) * kp, kp)
    a = hid[1, :, last]
    for n in range(tiles + 1):
        if n < tiles:
            here = slice(n * rt, (n + 1) * rt)
            part = jnp.dot(a, w_v[last, here], preferred_element_type=jnp.float32)
            acc[1, :, :, here] += part.reshape(n_pair, half, rt)
        if n > 0:

            @pl.when(core == 0)
            def _():
                swap(1, n - 1).start()

    @pl.when(core == 1)
    def _():
        load_res.wait()
        load_gain.wait()
        sum_pair(1)

    sums = jnp.zeros((half, 128), jnp.float32)
    gain = gain_v[...].astype(jnp.float32)
    writes = []
    for n in range(tiles):
        here = slice(n * rt, (n + 1) * rt)
        value = total[:, here]
        for step in range(1, n_pair):
            scatter(n, step).wait_recv()
            value = value + recv_buf[step - 1, :, here].astype(jnp.float32)
        total[:, here] = value
        square = value * value
        for j in range(rt // 128):
            lane = n * (rt // 128) + j
            sums = sums + square[:, j * 128 : (j + 1) * 128]
            pre[:, lane * 128 : (lane + 1) * 128] = (
                value[:, j * 128 : (j + 1) * 128] * gain[lane : lane + 1, :]
            )
        if n == tiles - 1:
            squares[z] = jnp.broadcast_to(jnp.sum(sums, axis=1, keepdims=True), sums.shape)

    def share(step):
        return pltpu.make_async_remote_copy(
            src_ref=squares.at[z],
            dst_ref=squares.at[z],
            send_sem=q_send.at[step - 1],
            recv_sem=q_recv.at[step - 1],
            device_id={"col": lax.rem(z + step, n_col)},
            device_id_type=MESH,
        )

    def arrival(step):
        block = squares.at[lax.rem(z + n_col - step, n_col)]
        return pltpu.make_async_remote_copy(
            src_ref=block,
            dst_ref=block,
            send_sem=q_send.at[step - 1],
            recv_sem=q_recv.at[step - 1],
            device_id={"col": lax.rem(z + step, n_col)},
            device_id_type=MESH,
        )

    for step in range(1, n_col):
        share(step).start()
    writes = [
        pltpu.make_async_copy(total, total_hbm, out_sem.at[0]),
        pltpu.make_async_copy(pre, pre_hbm, out_sem.at[1]),
    ]
    for write in writes:
        write.start()

    for source in range(n_col):
        block = hid.at[:, source * half : (source + 1) * half, :]
        for up in (0, 1):
            sent = jnp.logical_and(source >= z, z > 0)
            if up:
                sent = jnp.logical_and(source <= z, z < n_col - 1)

            @pl.when(sent)
            def _():
                pltpu.make_async_remote_copy(
                    src_ref=block,
                    dst_ref=block,
                    send_sem=ag_send.at[up, source],
                    recv_sem=ag_recv.at[source, 0, 0],
                    device_id={"col": z + 1 if up else z - 1},
                    device_id_type=MESH,
                ).wait_send()

    pltpu.make_async_remote_copy(
        src_ref=peer,
        dst_ref=peer,
        send_sem=d_send,
        recv_sem=d_recv.at[0],
        device_id={"tp": 2 * plane + 1 - core},
        device_id_type=MESH,
    ).wait_send()
    for step in range(1, n_pair):
        to = lax.rem(plane + step, n_pair)
        pltpu.make_async_remote_copy(
            src_ref=send_buf.at[to],
            dst_ref=recv_buf.at[step - 1],
            send_sem=r_send.at[step - 1],
            recv_sem=r_recv.at[step - 1, 0],
            device_id={"tp": 2 * to + core},
            device_id_type=MESH,
        ).wait_send()
    for write in writes:
        write.wait()
    for step in range(1, n_col):
        share(step).wait_send()
        arrival(step).wait_recv()
    whole = squares[0]
    for j in range(1, n_col):
        whole = whole + squares[j]
    scale_out[...] = lax.rsqrt(whole / width_all + EPS)


def finish(total_ref, pre_ref, scale_ref, stream_ref, normed_ref):
    stream_ref[...] = total_ref[...].astype(jnp.bfloat16)
    scale = scale_ref[...]
    for j in range(total_ref.shape[1] // 128):
        here = slice(j * 128, (j + 1) * 128)
        normed_ref[:, here] = (pre_ref[:, here] * scale).astype(jnp.bfloat16)


def fused_body(n_tp, n_col, kp, nt, rt, width, gate_in, up_in, down_weight, residual, norm_gain):
    rows, depth = gate_in.shape
    local = down_weight.shape[1]
    half = residual.shape[0]
    n_pair = n_tp // 2
    pieces, tiles = depth // kp, local // rt
    any_space = pl.BlockSpec(memory_space=pl.ANY)
    vmem = pl.BlockSpec(memory_space=pltpu.VMEM)
    dma = pltpu.SemaphoreType.DMA
    block32 = jax.ShapeDtypeStruct((half, local), jnp.float32)
    total, pre, scale = pl.pallas_call(
        functools.partial(kernel, n_col, n_pair, kp, nt, rt, SKEW, SPLIT, width),
        out_shape=(block32, block32, jax.ShapeDtypeStruct((half, 128), jnp.float32)),
        in_specs=[any_space] * 5,
        out_specs=(any_space, any_space, vmem),
        scratch_shapes=[
            pltpu.VMEM((rows, depth), jnp.bfloat16),
            pltpu.VMEM((rows, depth), jnp.bfloat16),
            pltpu.VMEM((2, half * n_col, depth), jnp.bfloat16),
            pltpu.VMEM((depth, local), jnp.bfloat16),
            pltpu.VMEM((2, n_pair, half, local), jnp.float32),
            pltpu.VMEM((n_pair, half, local), jnp.float32),
            pltpu.VMEM((n_pair, half, local), jnp.bfloat16),
            pltpu.VMEM((n_pair - 1, half, local), jnp.bfloat16),
            pltpu.VMEM((half, local), jnp.float32),
            pltpu.VMEM((half, local), jnp.float32),
            pltpu.VMEM((half, local), jnp.bfloat16),
            pltpu.VMEM((local // 128, 128), jnp.bfloat16),
            pltpu.VMEM((n_col, half, 128), jnp.float32),
            dma((2, pieces)),
            dma((pieces,)),
            dma,
            dma,
            dma((2,)),
            dma((2, n_col)),
            dma((n_col, 2, pieces)),
            dma,
            dma((tiles,)),
            dma((n_pair - 1,)),
            dma((n_pair - 1, tiles)),
            dma((n_col - 1,)),
            dma((n_col - 1,)),
        ],
        compiler_params=pltpu.CompilerParams(
            collective_id=0, has_side_effects=True, vmem_limit_bytes=VMEM_BYTES
        ),
        name="down_reduce",
    )(gate_in, up_in, down_weight, residual, norm_gain.reshape(-1, 128))
    out = jax.ShapeDtypeStruct((half, local), jnp.bfloat16)
    return pl.pallas_call(
        finish, out_shape=(out, out), in_specs=[vmem] * 3, out_specs=(vmem, vmem), name="finish"
    )(total, pre, scale)


def pairs_share_chip(mesh):
    if tuple(mesh.axis_names) != ("tp", "col") or mesh.shape["tp"] % 2 or mesh.shape["tp"] < 4:
        return False
    devices = mesh.devices
    for j in range(0, mesh.shape["tp"], 2):
        for a, b in zip(devices[j], devices[j + 1]):
            first = getattr(a, "coords", None)
            if first is None or list(first) != list(getattr(b, "coords", ())):
                return False
    return True


def solution(mesh):
    in_specs = (P("col", "tp"), P("col", "tp"), P("tp", "col"), P("tp", "col"), P("col"))
    out_specs = (P("tp", "col"), P("tp", "col"))
    n_tp, n_col = mesh.shape["tp"], mesh.shape["col"]

    def run(gate_in, up_in, down_weight, residual, norm_gain):
        tokens, hidden_units = gate_in.shape
        width = down_weight.shape[1]
        depth, local = hidden_units // n_tp, width // n_col
        rows, own_rows = tokens // n_col, tokens // n_tp
        kp, nt, rt = pick(depth, 512, 128), pick(local, 1024, 128), pick(local, 512, 128)
        need = 2 * depth * (local + tokens + 2 * rows) + local * tokens * 9 + (4 << 20)
        fused = (
            pairs_share_chip(mesh)
            and n_col > 1
            and rows % 16 == 0
            and own_rows % 16 == 0
            and rows == 2 * own_rows
            and n_tp == 2 * n_col
            and local % 1024 == 0
            and kp > 0
            and SKEW < SPLIT + 1 < depth // kp
            and nt > 0
            and need < VMEM_BYTES
        )
        body = functools.partial(plain_body, width)
        if fused:
            body = functools.partial(fused_body, n_tp, n_col, kp, nt, rt, width)
        return jax.shard_map(
            body, mesh=mesh, in_specs=in_specs, out_specs=out_specs, check_vma=False
        )(gate_in, up_in, down_weight, residual, norm_gain)

    return run
```

time: 54.2 us -> 51.4 us (0.948)
  other arithmetic: 3.9 us -> 0 us
  Pallas kernels: 49.1 us -> 50.6 us
    convert_element_type x2 -> x0, other arithmetic: 3.08 us -> none  [the longest x1 1.79 us: fused_body(): return (summed.astype(jnp.bfloat16), scaled.astype(jnp.bfloat16))]
    pallas_call x1 -> x2, Pallas kernels: 49.1 us -> 50.6 us  [the longest x1 48.8 us: fused_body(): pl.pallas_call(functools.partial(kernel, n_col, n_pair, kp, nt, rt, SKEW,...]
    rsqrt x1 -> x0, other arithmetic: 0.81 us -> none  [fused_body(): lax.rsqrt(mean_square + EPS)]
where the time goes in v1:
time: 51.4 us; the launch traced here: 51.2 us
  Pallas kernels  50.6 us (98%)
  between operations  0.64 us (1%)
    pallas_call x1, Pallas kernels, fused_body(): pl.pallas_call(functools.partial(kernel, n_col, n_pair, kp, nt, rt, SKEW,...  48.8 us
    pallas_call x1, Pallas kernels, fused_body(): pl.pallas_call(finish, out_shape=(out, out), in_specs=[vmem] * 3, out_spe...  1.75 us

profile of v1, /device:TPU:1, one launch (start us, length us, event | category | flops | bytes accessed | tf_op | source)
XLA Modules:
  0.0 51.2 jit_solution(10036947681923047400)
XLA Ops:
  0.6 48.8 %down_reduce.1 = (f32[16,4096]{1,0:T(8,128)}, f32[16,4096]{1,0:T(8,128)}, f32[16,128]{1,0:T(8,128)}) custom-call(bf16[32,6656]{1,0:T(8,128)(2,1)} %gate_hbm.1, bf16[32,6656]{1,0:T(8,128)(2,1)} %up_hbm.1, bf16[6656,4096]{1,0:T(8,128)(2,1)} %w_hbm.1, bf16[16,4096]{1,0:T(8,128)(2,1)} %res_hbm.1, bf16[32,128]{1,0:T(8,128)(2,1)} %bitcast.1), custom_call_target="tpu_custom_call" | custom-call | tf_op jit(solution)/shard_map/down_reduce/pallas_call | solution.py:403
  49.5 1.7 %finish.1 = (bf16[16,4096]{1,0:T(8,128)(2,1)}, bf16[16,4096]{1,0:T(8,128)(2,1)}) custom-call(f32[16,4096]{1,0:T(8,128)} %get-tuple-element.5.total_ref, f32[16,4096]{1,0:T(8,128)} %get-tuple-element.6.pre_ref, f32[16,128]{1,0:T(8,128)} %get-tuple-element.7.scale_ref), custom_call_target="tpu_custom_call" | custom-call | tf_op jit(solution)/shard_map/finish/pallas_call | solution.py:442

commit v2 on v1

--- a/solution.py
+++ b/solution.py
@@ -10,7 +10,7 @@
 MESH = pl.DeviceIdType.MESH
 VMEM_BYTES = 67_043_328
 EPS = 1e-05
-SKEW = 5
+SKEW = 4
 SPLIT = 5
 
 
@@ -46,7 +46,7 @@
     total_hbm, pre_hbm, scale_out,
     gate_v, up_v, hid, w_v, acc, peer, send_buf, recv_buf, total, pre, res_v, gain_v, squares,
     in_sem, w_sem, res_sem, gain_sem, out_sem,
-    ag_send, ag_recv, d_send, d_recv, r_send, r_recv, q_send, q_recv,
+    ag_send, ag_recv, d_send, d_recv, r_send, r_recv, q_send, q_recv, ready,
 ):
     depth = gate_hbm.shape[1]
     width = w_hbm.shape[1]
@@ -59,19 +59,34 @@
     z = lax.axis_index("col")
     plane, core = me // 2, lax.rem(me, 2)
 
+    below, above = z, n_col - 1 - z
+    few, many = jnp.minimum(below, above), jnp.maximum(below, above)
+    inward = jnp.where(below < above, 1, -1)
+    far_step = lax.rem(2 * n_pair - 1 - 2 * plane, n_pair)
+    beside = {"tp": 2 * plane + 1 - core}
+
+    def chip(step):
+        return {"tp": 2 * lax.rem(plane + step, n_pair) + core}
+
+    def tell(semaphore, device):
+        pl.semaphore_signal(semaphore, inc=1, device_id=device, device_id_type=MESH)
+
+    def tell_near(semaphore):
+        for step in range(1, n_pair):
+
+            @pl.when(step != far_step)
+            def _():
+                tell(semaphore, chip(step))
+
     barrier = pltpu.get_barrier_semaphore()
-    for step in range(1, n_col):
-        pl.semaphore_signal(
-            barrier, inc=1, device_id={"col": lax.rem(z + step, n_col)}, device_id_type=MESH
-        )
-    pl.semaphore_signal(barrier, inc=1, device_id={"tp": 2 * plane + 1 - core}, device_id_type=MESH)
-    for step in range(1, n_pair):
-        pl.semaphore_signal(
-            barrier,
-            inc=1,
-            device_id={"tp": 2 * lax.rem(plane + step, n_pair) + core},
-            device_id_type=MESH,
-        )
+    tell(barrier, {"col": z + inward})
+
+    @pl.when(few > 0)
+    def _():
+        tell(barrier, {"col": z - inward})
+
+    tell_near(barrier)
+    tell(barrier, beside)
 
     def cols(s):
         return pl.ds(pl.multiple_of(s * kp, kp), kp)
@@ -134,13 +149,11 @@
         def _():
             each(source, u, to, start)
 
-    below, above = z, n_col - 1 - z
-    few, many = jnp.minimum(below, above), jnp.maximum(below, above)
-    inward = jnp.where(below < above, 1, -1)
     lag = skew * jnp.maximum(many - 1, 0)
     lead = jnp.where(few > 0, skew, pieces)
 
-    pl.semaphore_wait(barrier, n_col - 1 + 1 + n_pair - 1)
+    pl.semaphore_wait(barrier, 1 + jnp.minimum(few, 1) + n_pair - 2 + 1)
+    tell_near(ready)
 
     @pl.loop(0, pieces + 1)
     def _(s):
@@ -175,7 +188,7 @@
             dst_ref=peer.at[:, :, here],
             send_sem=d_send,
             recv_sem=d_recv.at[n],
-            device_id={"tp": 2 * plane + 1 - core},
+            device_id=beside,
             device_id_type=MESH,
         )
 
@@ -192,6 +205,9 @@
         )
 
     def sum_pair(group):
+        load_res.wait()
+        load_gain.wait()
+        pl.semaphore_wait(ready, n_pair - 2)
         for n in range(tiles + 1):
             if n < tiles:
                 here = slice(n * rt, (n + 1) * rt)
@@ -205,8 +221,12 @@
                     + res_v[:, here].astype(jnp.float32)
                 )
             if n > 0:
+                scatter(n - 1, far_step).start()
                 for step in range(1, n_pair):
-                    scatter(n - 1, step).start()
+
+                    @pl.when(step != far_step)
+                    def _():
+                        scatter(n - 1, step).start()
 
     @pl.loop(0, units + skew * (n_col - 2))
     def _(i):
@@ -260,10 +280,8 @@
                 part = jnp.dot(a, w_v[cols(s), here], preferred_element_type=jnp.float32)
                 acc[group, :, :, here] += part.reshape(n_pair, half, nt)
 
-        @pl.when(jnp.logical_and(u == pieces + split // 2 + 1, core == 0))
-        def _():
-            load_res.wait()
-            load_gain.wait()
+        @pl.when(jnp.logical_and(u == pieces + split // 2, core == 0))
+        def _():
             sum_pair(0)
 
     last = pl.ds((pieces - 1) * kp, kp)
@@ -281,8 +299,6 @@
 
     @pl.when(core == 1)
     def _():
-        load_res.wait()
-        load_gain.wait()
         sum_pair(1)
 
     sums = jnp.zeros((half, 128), jnp.float32)
@@ -358,7 +374,7 @@
         dst_ref=peer,
         send_sem=d_send,
         recv_sem=d_recv.at[0],
-        device_id={"tp": 2 * plane + 1 - core},
+        device_id=beside,
         device_id_type=MESH,
     ).wait_send()
     for step in range(1, n_pair):
@@ -432,6 +448,7 @@
             dma((n_pair - 1, tiles)),
             dma((n_col - 1,)),
             dma((n_col - 1,)),
+            pltpu.SemaphoreType.REGULAR,
         ],
         compiler_params=pltpu.CompilerParams(
             collective_id=0, has_side_effects=True, vmem_limit_bytes=VMEM_BYTES

time: 51.4 us -> 50.3 us (0.979)
  Pallas kernels: 50.6 us -> 49.6 us
    pallas_call x1, Pallas kernels: 48.8 us -> 47.8 us  [fused_body(): pl.pallas_call(functools.partial(kernel, n_col, n_pair, kp, nt, rt, SKEW,...]
where the time goes in v2:
time: 50.3 us; the launch traced here: 50.2 us
  Pallas kernels  49.6 us (99%)
  between operations  0.64 us (1%)
    pallas_call x1, Pallas kernels, fused_body(): pl.pallas_call(functools.partial(kernel, n_col, n_pair, kp, nt, rt, SKEW,...  47.8 us
    pallas_call x1, Pallas kernels, fused_body(): pl.pallas_call(finish, out_shape=(out, out), in_specs=[vmem] * 3, out_spe...  1.75 us

profile of v2, /device:TPU:1, one launch (start us, length us, event | category | flops | bytes accessed | tf_op | source)
XLA Modules:
  0.0 50.2 jit_solution(9673743249873217555)
XLA Ops:
  0.6 47.8 %down_reduce.1 = (f32[16,4096]{1,0:T(8,128)}, f32[16,4096]{1,0:T(8,128)}, f32[16,128]{1,0:T(8,128)}) custom-call(bf16[32,6656]{1,0:T(8,128)(2,1)} %gate_hbm.1, bf16[32,6656]{1,0:T(8,128)(2,1)} %up_hbm.1, bf16[6656,4096]{1,0:T(8,128)(2,1)} %w_hbm.1, bf16[16,4096]{1,0:T(8,128)(2,1)} %res_hbm.1, bf16[32,128]{1,0:T(8,128)(2,1)} %bitcast.1), custom_call_target="tpu_custom_call" | custom-call | tf_op jit(solution)/shard_map/down_reduce/pallas_call | solution.py:419
  48.4 1.7 %finish.1 = (bf16[16,4096]{1,0:T(8,128)(2,1)}, bf16[16,4096]{1,0:T(8,128)(2,1)}) custom-call(f32[16,4096]{1,0:T(8,128)} %get-tuple-element.5.total_ref, f32[16,4096]{1,0:T(8,128)} %get-tuple-element.6.pre_ref, f32[16,128]{1,0:T(8,128)} %get-tuple-element.7.scale_ref), custom_call_target="tpu_custom_call" | custom-call | tf_op jit(solution)/shard_map/finish/pallas_call | solution.py:459
